TPU v7x, 32 devices: a whole 2x2x4 slice. The times are simulated.
32 devices in a mesh: wide: 8 (over z, y), narrow: 4 (over x, core).
Axes of the slice: x: 2, y: 2, z: 4, core: 2. Of those that a mesh axis runs over, the one named last changes fastest.
Arguments:
- queries: bfloat16 [2048, 1024], P(('wide', 'narrow')), may hold values from -16 to 16
- documents: bfloat16 [2048, 1024], P(('wide', 'narrow')), may hold values from -16 to 16
- user_ids: int32 [2048], replicated, may hold values from 0 to 1663, as said below
Outputs:
- query_grad: bfloat16 [2048, 1024], P(('wide', 'narrow'))
- doc_grad: bfloat16 [2048, 1024], P(('wide', 'narrow'))
- loss: float32 [], replicated
Inputs may be any that keep to these rules, and one draw needn't show every extreme that they name: `user_ids`: each user id names at most 4 rows; rows with a common id lie in the same quarter of the 2048 rows.
All inputs are finite; a program needn't handle non-finite values.
Results may differ from a plain program's by a relative error of at most 0.004.
The roundings to bfloat16 on the way count: a program that leaves them out, or rounds other values in their place, can miss the bound.
Values may be sent and summed in bfloat16 or wider, within the bound.
No kernel may reach another device: no remote copies, remote signals or barrier semaphores. Data moves between devices by JAX's collectives and lax.ppermute only.
A program may use at most 64 MiB of HBM per device.

v0:
```python
import math
import jax
import jax.numpy as jnp
from jax import lax
from jax.sharding import PartitionSpec as P


def passed_along(array, axis, by):
    devices = lax.axis_size(axis)
    return lax.ppermute(array, axis, [(i, (i + by) % devices) for i in range(devices)])


def local(queries, documents, user_ids):
    wide_count = lax.axis_size("wide")
    narrow_count = lax.axis_size("narrow")
    own_rows = queries.shape[0]
    width = queries.shape[1]
    wide_index = lax.axis_index("wide")
    narrow_index = lax.axis_index("narrow")
    score_scale = 3.0 / math.sqrt(width)
    batch_rows = jnp.float32(wide_count * narrow_count * own_rows)
    group_queries = lax.all_gather(queries, "narrow", axis=0, tiled=True)
    group_docs = lax.all_gather(documents, "wide", axis=0, tiled=True)
    id_table = user_ids.reshape(wide_count, narrow_count, own_rows)
    query_users = lax.dynamic_index_in_dim(id_table, wide_index, 0, keepdims=False).reshape(-1)
    doc_users = lax.dynamic_index_in_dim(id_table, narrow_index, 1, keepdims=False).reshape(-1)
    positive = query_users[:, None] == doc_users[None, :]
    positive_float = positive.astype(jnp.float32)
    counts_local = jnp.sum(positive_float, axis=1)
    scores = (
        lax.dot_general(
            group_queries, group_docs, (((1,), (1,)), ((), ())), preferred_element_type=jnp.float32
        )
        * score_scale
    )
    pos_local = jnp.sum(jnp.where(positive, scores, jnp.float32(0.0)), axis=1)
    local_peak = jnp.max(scores, axis=1)
    row_peak = lax.pmax(local_peak, "narrow")
    local_denom = jnp.sum(jnp.exp(scores - row_peak[:, None]), axis=1)
    row_denom, counts, pos_sum = lax.psum((local_denom, counts_local, pos_local), "narrow")
    log_denom = row_peak + jnp.log(row_denom)
    row_terms = counts * log_denom - pos_sum
    total, loss_sum = lax.psum((jnp.sum(counts), jnp.sum(row_terms)), "wide")
    probs = jnp.exp(scores - log_denom[:, None])
    weights = (batch_rows * (counts[:, None] * probs - positive_float) / total).astype(jnp.bfloat16)

    def doc_term(first_row, row_count):
        cols_block = lax.dynamic_slice_in_dim(weights, first_row, row_count, 1)
        return (
            lax.dot_general(
                cols_block,
                group_queries,
                (((0,), (0,)), ((), ())),
                preferred_element_type=jnp.float32,
            )
            * score_scale
        )

    query_grad = lax.psum_scatter(
        jnp.dot(weights, group_docs, preferred_element_type=jnp.float32) * score_scale,
        "narrow",
        scatter_dimension=0,
        tiled=True,
    )

    def block_term(block_number):
        start = jnp.mod(block_number, wide_count) * own_rows
        return doc_term(start, own_rows)

    def advance(turn, partial_sum):
        passed = passed_along(partial_sum, "wide", 1)
        return passed + block_term(wide_index - 1 - turn + wide_count)

    doc_grad = lax.fori_loop(1, wide_count, advance, block_term(wide_index - 1 + wide_count))
    return (query_grad.astype(jnp.bfloat16), doc_grad.astype(jnp.bfloat16), loss_sum / total)


def solution(mesh):
    return jax.shard_map(
        local,
        mesh=mesh,
        in_specs=(P(("wide", "narrow"), None), P(("wide", "narrow"), None), P()),
        out_specs=(P(("wide", "narrow"), None), P(("wide", "narrow"), None), P()),
        check_vma=False,
    )
```

profile of v0, /device:TPU:0, one launch (start us, length us, event | category | flops | bytes accessed | tf_op | source)
XLA Modules:
  0.0 175.9 jit_solution(14605701995390080178)
XLA Ops:
  7.2 0.0 copy-start.1
  7.2 0.0 all-gather.2.cloned.1.call-start
  7.2 0.7 all-gather.2.cloned.1.call-update
  7.9 0.0 copy-start.2
  7.9 0.0 reduce-scatter.2.cloned.1.call-start
  8.0 0.6 copy-done.2
  8.6 0.1 reshape.16
  8.7 0.1 eq.26
  8.8 0.1 eq.28
  8.9 0.0 copy-done.1
  8.9 8.6 %all_gather.6 = bf16[256,1024]{1,0:T(8,128)(2,1)S(1)} all-gather(bf16[64,1024]{1,0:T(8,128)(2,1)S(1)} %copy-done.1), channel_id=1, replica_groups=mesh['wide'=8,'narrow'=4] {'narrow'}, dimensions={0}, use_global_device_ids=true | all-gather | bytes 655360 | tf_op jit(solution)/shard_map/all_gather | solution.py:22
  17.5 35.6 %all-gather.2.cloned.1.call-done = bf16[512,1024]{1,0:T(8,128)(2,1)} async-done(((bf16[64,1024]{1,0:T(8,128)(2,1)}), bf16[512,1024]{1,0:T(8,128)(2,1)}) %all-gather.2.cloned.1.call-update) | async-done | bytes 1048592 | tf_op jit(solution)/shard_map/all_gather | solution.py:23
  53.2 1.8 %fusion.9 = (f32[256]{0:T(256)S(1)}, f32[256,512]{1,0:T(8,128)S(1)}) fusion(bf16[256,1024]{1,0:T(8,128)(2,1)S(1)} %all_gather.6, bf16[512,1024]{1,0:T(8,128)(2,1)} %all-gather.2.cloned.1.call-done), kind=kOutput, calls=%fused_computation.21 | convolution fusion | flops 268697344 | bytes 2098176 | tf_op jit(solution)/shard_map/dot_general | solution.py:31
  54.9 0.0 copy-start
  54.9 5.8 %pmax.7 = f32[256]{0:T(256)S(1)} all-reduce(f32[256]{0:T(256)S(1)} %get-tuple-element.161), channel_id=1, replica_groups=mesh['wide'=8,'narrow'=4] {'narrow'}, use_global_device_ids=true, to_apply=%region_3.4 | all-reduce | flops 256 | bytes 2048 | tf_op jit(solution)/shard_map/pmax | solution.py:38
  60.7 0.3 fusion.3
  61.1 6.6 %all-reduce.1 = (f32[256]{0:T(256)S(1)}, f32[256]{0:T(256)S(1)}, f32[256]{0:T(256)S(1)}) all-reduce(f32[256]{0:T(256)S(1)} %get-tuple-element.140, f32[256]{0:T(256)S(1)} %get-tuple-element.142, f32[256]{0:T(256)S(1)} %get-tuple-element.141), channel_id=1, replica_groups=mesh['wide'=8,'narrow'=4] {'narrow'}, use_global_device_ids=true, to_apply=%region_12.13 | all-reduce | flops 768 | bytes 6144 | tf_op jit(solution)/shard_map/psum | solution.py:40
  67.7 0.6 subtract_reduce_fusion
  68.3 19.8 %all-reduce = (f32[]{:T(128)}, f32[]{:T(128)}) all-reduce(f32[]{:T(128)} %get-tuple-element.144, f32[]{:T(128)} %get-tuple-element.143), channel_id=1, replica_groups=mesh['wide'=8,'narrow'=4] {'wide'}, use_global_device_ids=true, to_apply=%region_7.8 | all-reduce | flops 2 | bytes 16 | tf_op jit(solution)/shard_map/psum | solution.py:43
  88.1 0.9 fusion.6
  89.0 0.0 copy-done
  89.0 1.4 convolution_multiply_fusion.1
  90.4 0.0 reduce-scatter.2.cloned.1.call-update
  90.4 0.3 convolution_multiply_fusion.3
  90.8 73.5 %while.15 = (s32[]{:T(128)}, f32[64,1024]{1,0:T(8,128)S(1)}, s32[]{:T(128)}, bf16[256,512]{1,0:T(8,128)(2,1)S(1)}, bf16[256,1024]{1,0:T(8,128)(2,1)S(1)}, /*inde...) while((s32[]{:T(128)}, f32[64,1024]{1,0:T(8,128)S(1)}, s32[]{:T(128)}, ...), condition=%wide.region_10.11_spmd, body=%wide.region_9.10_spmd.sunk | while | flops 33685520 | bytes 2163020 | solution.py:74
  90.8 0.1 collective-permute-start
  90.9 9.2 %collective-permute-done = f32[64,1024]{1,0:T(8,128)S(1)} collective-permute-done((f32[64,1024]{1,0:T(8,128)S(1)}, f32[64,1024]{1,0:T(8,128)S(1)}, u32[]{:S(2)}, u32[]{:S(2)}) %collective-permute-start) | collective-permute-done | bytes 262176 | tf_op jit(solution)/shard_map/while/body/eval_jaxpr/ppermute | solution.py:10
  100.1 0.3 fusion.21
  100.4 0.1 collective-permute-start
  100.5 10.4 %collective-permute-done = f32[64,1024]{1,0:T(8,128)S(1)} collective-permute-done((f32[64,1024]{1,0:T(8,128)S(1)}, f32[64,1024]{1,0:T(8,128)S(1)}, u32[]{:S(2)}, u32[]{:S(2)}) %collective-permute-start) | collective-permute-done | bytes 262176 | tf_op jit(solution)/shard_map/while/body/eval_jaxpr/ppermute | solution.py:10
  110.9 0.3 fusion.21
  111.2 0.1 collective-permute-start
  111.3 11.5 %collective-permute-done = f32[64,1024]{1,0:T(8,128)S(1)} collective-permute-done((f32[64,1024]{1,0:T(8,128)S(1)}, f32[64,1024]{1,0:T(8,128)S(1)}, u32[]{:S(2)}, u32[]{:S(2)}) %collective-permute-start) | collective-permute-done | bytes 262176 | tf_op jit(solution)/shard_map/while/body/eval_jaxpr/ppermute | solution.py:10
  122.8 0.3 fusion.21
  123.2 0.1 collective-permute-start
  123.3 11.0 %collective-permute-done = f32[64,1024]{1,0:T(8,128)S(1)} collective-permute-done((f32[64,1024]{1,0:T(8,128)S(1)}, f32[64,1024]{1,0:T(8,128)S(1)}, u32[]{:S(2)}, u32[]{:S(2)}) %collective-permute-start) | collective-permute-done | bytes 262176 | tf_op jit(solution)/shard_map/while/body/eval_jaxpr/ppermute | solution.py:10
  134.3 0.3 fusion.21
  134.6 0.1 collective-permute-start
  134.7 10.1 %collective-permute-done = f32[64,1024]{1,0:T(8,128)S(1)} collective-permute-done((f32[64,1024]{1,0:T(8,128)S(1)}, f32[64,1024]{1,0:T(8,128)S(1)}, u32[]{:S(2)}, u32[]{:S(2)}) %collective-permute-start) | collective-permute-done | bytes 262176 | tf_op jit(solution)/shard_map/while/body/eval_jaxpr/ppermute | solution.py:10
  144.8 0.3 fusion.21
  145.1 0.1 collective-permute-start
  145.2 9.3 %collective-permute-done = f32[64,1024]{1,0:T(8,128)S(1)} collective-permute-done((f32[64,1024]{1,0:T(8,128)S(1)}, f32[64,1024]{1,0:T(8,128)S(1)}, u32[]{:S(2)}, u32[]{:S(2)}) %collective-permute-start) | collective-permute-done | bytes 262176 | tf_op jit(solution)/shard_map/while/body/eval_jaxpr/ppermute | solution.py:10
  154.5 0.3 fusion.21
  154.8 0.1 collective-permute-start
  154.9 9.0 %collective-permute-done = f32[64,1024]{1,0:T(8,128)S(1)} collective-permute-done((f32[64,1024]{1,0:T(8,128)S(1)}, f32[64,1024]{1,0:T(8,128)S(1)}, u32[]{:S(2)}, u32[]{:S(2)}) %collective-permute-start) | collective-permute-done | bytes 262176 | tf_op jit(solution)/shard_map/while/body/eval_jaxpr/ppermute | solution.py:10
  164.0 0.3 fusion.21
  164.3 0.7 convert_element_type.15
  166.3 0.0 reduce-scatter.2.cloned.1.call-done
  166.3 1.6 convert_element_type.14
  (2 shorter events, 0.0 us)
Async XLA Ops:
  7.2 1.7 copy-start.1
  7.2 46.0 %all-gather.2.cloned.1.call-start = ((), (), s32[]{:S(2)}) async-start(), calls=%async_computation.1 | async-start | bytes 1179648 | tf_op jit(solution)/shard_map/all_gather | solution.py:23
  7.9 0.7 copy-start.2
  7.9 158.4 %reduce-scatter.2.cloned.1.call-start = ((), (), s32[]{:S(2)}) async-start(), calls=%async_computation.2 | async-start | bytes 1310720 | tf_op jit(solution)/shard_map/reduce_scatter | solution.py:59
  54.9 34.0 %copy-start = (bf16[512,1024]{1,0:T(8,128)(2,1)S(1)}, bf16[512,1024]{1,0:T(8,128)(2,1)}, u32[]{:S(2)}) copy-start(bf16[512,1024]{1,0:T(8,128)(2,1)} %all-gather.2.cloned.1.call-done) | copy-start | bytes 3145732
  90.8 9.3 %collective-permute-start = (f32[64,1024]{1,0:T(8,128)S(1)}, f32[64,1024]{1,0:T(8,128)S(1)}, u32[]{:S(2)}, u32[]{:S(2)}) collective-permute-start(f32[64,1024]{1,0:T(8,128)S(1)} %get-tuple-element.206), channel_id=1, source_target_pairs={{0,4},{4,8},{8,12},{12,16},{16,20},{20,24},{24,28},{28,0},{1,5},{5... | collective-permute-start | bytes 786440 | tf_op jit(solution)/shard_map/while/body/eval_jaxpr/ppermute | solution.py:10
  100.4 10.5 %collective-permute-start = (f32[64,1024]{1,0:T(8,128)S(1)}, f32[64,1024]{1,0:T(8,128)S(1)}, u32[]{:S(2)}, u32[]{:S(2)}) collective-permute-start(f32[64,1024]{1,0:T(8,128)S(1)} %get-tuple-element.206), channel_id=1, source_target_pairs={{0,4},{4,8},{8,12},{12,16},{16,20},{20,24},{24,28},{28,0},{1,5},{5... | collective-permute-start | bytes 786440 | tf_op jit(solution)/shard_map/while/body/eval_jaxpr/ppermute | solution.py:10
  111.2 11.6 %collective-permute-start = (f32[64,1024]{1,0:T(8,128)S(1)}, f32[64,1024]{1,0:T(8,128)S(1)}, u32[]{:S(2)}, u32[]{:S(2)}) collective-permute-start(f32[64,1024]{1,0:T(8,128)S(1)} %get-tuple-element.206), channel_id=1, source_target_pairs={{0,4},{4,8},{8,12},{12,16},{16,20},{20,24},{24,28},{28,0},{1,5},{5... | collective-permute-start | bytes 786440 | tf_op jit(solution)/shard_map/while/body/eval_jaxpr/ppermute | solution.py:10
  123.2 11.1 %collective-permute-start = (f32[64,1024]{1,0:T(8,128)S(1)}, f32[64,1024]{1,0:T(8,128)S(1)}, u32[]{:S(2)}, u32[]{:S(2)}) collective-permute-start(f32[64,1024]{1,0:T(8,128)S(1)} %get-tuple-element.206), channel_id=1, source_target_pairs={{0,4},{4,8},{8,12},{12,16},{16,20},{20,24},{24,28},{28,0},{1,5},{5... | collective-permute-start | bytes 786440 | tf_op jit(solution)/shard_map/while/body/eval_jaxpr/ppermute | solution.py:10
  134.6 10.2 %collective-permute-start = (f32[64,1024]{1,0:T(8,128)S(1)}, f32[64,1024]{1,0:T(8,128)S(1)}, u32[]{:S(2)}, u32[]{:S(2)}) collective-permute-start(f32[64,1024]{1,0:T(8,128)S(1)} %get-tuple-element.206), channel_id=1, source_target_pairs={{0,4},{4,8},{8,12},{12,16},{16,20},{20,24},{24,28},{28,0},{1,5},{5... | collective-permute-start | bytes 786440 | tf_op jit(solution)/shard_map/while/body/eval_jaxpr/ppermute | solution.py:10
  145.1 9.4 %collective-permute-start = (f32[64,1024]{1,0:T(8,128)S(1)}, f32[64,1024]{1,0:T(8,128)S(1)}, u32[]{:S(2)}, u32[]{:S(2)}) collective-permute-start(f32[64,1024]{1,0:T(8,128)S(1)} %get-tuple-element.206), channel_id=1, source_target_pairs={{0,4},{4,8},{8,12},{12,16},{16,20},{20,24},{24,28},{28,0},{1,5},{5... | collective-permute-start | bytes 786440 | tf_op jit(solution)/shard_map/while/body/eval_jaxpr/ppermute | solution.py:10
  154.8 9.1 %collective-permute-start = (f32[64,1024]{1,0:T(8,128)S(1)}, f32[64,1024]{1,0:T(8,128)S(1)}, u32[]{:S(2)}, u32[]{:S(2)}) collective-permute-start(f32[64,1024]{1,0:T(8,128)S(1)} %get-tuple-element.206), channel_id=1, source_target_pairs={{0,4},{4,8},{8,12},{12,16},{16,20},{20,24},{24,28},{28,0},{1,5},{5... | collective-permute-start | bytes 786440 | tf_op jit(solution)/shard_map/while/body/eval_jaxpr/ppermute | solution.py:10
Sparse Core Ops, SparseCore 0:
  10.1 42.9 all-gather.1
  90.5 21.4 reduce-scatter.1
where the time goes:
time: 176 us
  waiting for transfers between devices  107 us (61%)
  blocking collectives  40.8 us (23%)
  between operations  16.6 us (9%)
  matrix products  5.65 us (3%)
  other arithmetic  4.13 us (2%)
    ppermute x7, waiting for transfers between devices, passed_along(): lax.ppermute(array, axis, [(i, (i + by) % devices) for i in range(devices)])  70.6 us
    all_gather x1, waiting for transfers between devices, local(): group_docs = lax.all_gather(documents, 'wide', axis=0, tiled=True)  35.6 us
    psum x1, blocking collectives, local(): total, loss_sum = lax.psum((jnp.sum(counts), jnp.sum(row_terms)), 'wide')  19.8 us
    all_gather x1, blocking collectives, local(): group_queries = lax.all_gather(queries, 'narrow', axis=0, tiled=True)  8.63 us
    psum x1, blocking collectives, local(): lax.psum((local_denom, counts_local, pos_local), 'narrow')  6.59 us
    pmax x1, blocking collectives, local(): row_peak = lax.pmax(local_peak, 'narrow')  5.8 us
  transfers between devices with their start and end apart: 9, of which 8 were waited for; matrix products, arithmetic and copies ran while one was open for 2% of the time, Pallas kernels for 0%

commit v1 on v0

--- a/solution.py
+++ b/solution.py
@@ -20,7 +20,14 @@
     score_scale = 3.0 / math.sqrt(width)
     batch_rows = jnp.float32(wide_count * narrow_count * own_rows)
     group_queries = lax.all_gather(queries, "narrow", axis=0, tiled=True)
-    group_docs = lax.all_gather(documents, "wide", axis=0, tiled=True)
+    count = lax.axis_size("wide")
+    right = [(i_2, (i_2 + 1) % count) for i_2 in range(count)]
+    parts = [documents]
+    for far in range(1, count):
+        parts = [lax.ppermute(parts[0], "wide", right), *parts]
+    whole = jnp.concatenate(parts, axis=0)
+    turn_2 = (lax.axis_index("wide") + 1) * parts[-1].shape[0]
+    group_docs = jnp.roll(whole, turn_2, axis=0)
     id_table = user_ids.reshape(wide_count, narrow_count, own_rows)
     query_users = lax.dynamic_index_in_dim(id_table, wide_index, 0, keepdims=False).reshape(-1)
     doc_users = lax.dynamic_index_in_dim(id_table, narrow_index, 1, keepdims=False).reshape(-1)

time: 176 us -> 188 us (1.068)
  waiting for transfers between devices: 107 us -> 116 us
  starting transfers between devices: 0.49 us -> 3.51 us
  matrix products: 5.65 us -> 3.62 us
    ppermute x0 -> x7, waiting for transfers between devices: none -> 45.3 us  [local(): parts = [lax.ppermute(parts[0], 'wide', right), *parts]]
    all_gather x1 -> x0, waiting for transfers between devices: 35.6 us -> none  [local(): group_docs = lax.all_gather(documents, 'wide', axis=0, tiled=True)]
    ppermute x0 -> x7, starting transfers between devices: none -> 3.06 us  [local(): parts = [lax.ppermute(parts[0], 'wide', right), *parts]]
    psum x1, blocking collectives: 19.8 us -> 22 us  [local(): total, loss_sum = lax.psum((jnp.sum(counts), jnp.sum(row_terms)), 'wide')]
  transfers between devices with their start and end apart: 9 -> 15, of which waited for: 8 -> 13; matrix products, arithmetic and copies ran while one was open for 2% -> 2% of each run, Pallas kernels for 0% -> 0%
where the time goes in v1:
time: 188 us
  waiting for transfers between devices  116 us (62%)
  blocking collectives  42.2 us (22%)
  between operations  16.7 us (9%)
  other arithmetic  3.92 us (2%)
  matrix products  3.62 us (2%)
  starting transfers between devices  3.51 us (2%)
    ppermute x7, waiting for transfers between devices, passed_along(): lax.ppermute(array, axis, [(i, (i + by) % devices) for i in range(devices)])  71.1 us
    ppermute x7, waiting for transfers between devices, local(): parts = [lax.ppermute(parts[0], 'wide', right), *parts]  45.3 us
    psum x1, blocking collectives, local(): total, loss_sum = lax.psum((jnp.sum(counts), jnp.sum(row_terms)), 'wide')  22 us
    all_gather x1, blocking collectives, local(): group_queries = lax.all_gather(queries, 'narrow', axis=0, tiled=True)  7.7 us
    pmax x1, blocking collectives, local(): row_peak = lax.pmax(local_peak, 'narrow')  6.42 us
    psum x1, blocking collectives, local(): lax.psum((local_denom, counts_local, pos_local), 'narrow')  6.15 us
  transfers between devices with their start and end apart: 15, of which 13 were waited for; matrix products, arithmetic and copies ran while one was open for 2% of the time, Pallas kernels for 0%

profile of v1, /device:TPU:0, one launch (start us, length us, event | category | flops | bytes accessed | tf_op | source)
XLA Modules:
  0.0 188.0 jit_solution(5212989934229001363)
XLA Ops:
  7.2 0.0 copy-start
  7.2 0.0 reduce-scatter.2.cloned.1.call-start
  7.2 3.0 %collective-permute-start.1 = (bf16[64,1024]{1,0:T(8,128)(2,1)}, bf16[64,1024]{1,0:T(8,128)(2,1)S(1)}, u32[]{:S(2)}, u32[]{:S(2)}) collective-permute-start(bf16[64,1024]{1,0:T(8,128)(2,1)} %param.6), channel_id=1, source_target_pairs={{0,4},{4,8},{8,12},{12,16},{16,20},{20,24},{24,28},{28,0},{1,5},{5... | collective-permute-start | bytes 393224 | tf_op jit(solution)/shard_map/ppermute | solution.py:27
  10.3 6.7 %collective-permute-done.1 = bf16[64,1024]{1,0:T(8,128)(2,1)S(1)} collective-permute-done((bf16[64,1024]{1,0:T(8,128)(2,1)}, bf16[64,1024]{1,0:T(8,128)(2,1)S(1)}, u32[]{:S(2)}, u32[]{:S(2)}) %collective-permute-start.1) | collective-permute-done | bytes 131104 | tf_op jit(solution)/shard_map/ppermute | solution.py:27
  17.0 0.0 collective-permute-start.2
  17.0 7.7 %collective-permute-done.2 = bf16[64,1024]{1,0:T(8,128)(2,1)S(1)} collective-permute-done((bf16[64,1024]{1,0:T(8,128)(2,1)S(1)}, bf16[64,1024]{1,0:T(8,128)(2,1)S(1)}, u32[]{:S(2)}, u32[]{:S(2)}) %collective-permute-start.2) | collective-permute-done | bytes 131104 | tf_op jit(solution)/shard_map/ppermute | solution.py:27
  24.7 0.0 collective-permute-start.3
  24.7 7.7 %collective-permute-done.3 = bf16[64,1024]{1,0:T(8,128)(2,1)S(1)} collective-permute-done((bf16[64,1024]{1,0:T(8,128)(2,1)S(1)}, bf16[64,1024]{1,0:T(8,128)(2,1)S(1)}, u32[]{:S(2)}, u32[]{:S(2)}) %collective-permute-start.3) | collective-permute-done | bytes 131104 | tf_op jit(solution)/shard_map/ppermute | solution.py:27
  32.3 0.0 collective-permute-start.4
  32.3 7.7 %collective-permute-done.4 = bf16[64,1024]{1,0:T(8,128)(2,1)S(1)} collective-permute-done((bf16[64,1024]{1,0:T(8,128)(2,1)S(1)}, bf16[64,1024]{1,0:T(8,128)(2,1)S(1)}, u32[]{:S(2)}, u32[]{:S(2)}) %collective-permute-start.4) | collective-permute-done | bytes 131104 | tf_op jit(solution)/shard_map/ppermute | solution.py:27
  40.0 0.0 collective-permute-start.5
  40.0 7.7 %collective-permute-done.5 = bf16[64,1024]{1,0:T(8,128)(2,1)S(1)} collective-permute-done((bf16[64,1024]{1,0:T(8,128)(2,1)S(1)}, bf16[64,1024]{1,0:T(8,128)(2,1)S(1)}, u32[]{:S(2)}, u32[]{:S(2)}) %collective-permute-start.5) | collective-permute-done | bytes 131104 | tf_op jit(solution)/shard_map/ppermute | solution.py:27
  47.7 0.0 collective-permute-start.6
  47.7 0.8 reshape.16
  48.5 0.1 eq.29
  48.6 0.1 eq.31
  48.7 7.9 %collective-permute-done.6 = bf16[64,1024]{1,0:T(8,128)(2,1)S(1)} collective-permute-done((bf16[64,1024]{1,0:T(8,128)(2,1)S(1)}, bf16[64,1024]{1,0:T(8,128)(2,1)S(1)}, u32[]{:S(2)}, u32[]{:S(2)}) %collective-permute-start.6) | collective-permute-done | bytes 131104 | tf_op jit(solution)/shard_map/ppermute | solution.py:27
  56.6 0.0 collective-permute-start.7
  56.6 7.7 %all_gather.3 = bf16[256,1024]{1,0:T(8,128)(2,1)S(1)} all-gather(bf16[64,1024]{1,0:T(8,128)(2,1)} %param.5), channel_id=1, replica_groups=mesh['wide'=8,'narrow'=4] {'narrow'}, dimensions={0}, use_global_device_ids=true | all-gather | bytes 655360 | tf_op jit(solution)/shard_map/all_gather | solution.py:22
  64.3 0.0 collective-permute-done.7
  64.4 0.0 copy-done
  64.6 0.5 fusion.17
  65.1 6.4 %pmax.7 = f32[256]{0:T(256)S(1)} all-reduce(f32[256]{0:T(256)S(1)} %get-tuple-element.166), channel_id=1, replica_groups=mesh['wide'=8,'narrow'=4] {'narrow'}, use_global_device_ids=true, to_apply=%region_3.4 | all-reduce | flops 256 | bytes 2048 | tf_op jit(solution)/shard_map/pmax | solution.py:45
  71.5 0.2 fusion.5
  71.7 6.1 %all-reduce.1 = (f32[256]{0:T(256)S(1)}, f32[256]{0:T(256)S(1)}, f32[256]{0:T(256)S(1)}) all-reduce(f32[256]{0:T(256)S(1)} %get-tuple-element.145, f32[256]{0:T(256)S(1)} %get-tuple-element.147, f32[256]{0:T(256)S(1)} %get-tuple-element.146), channel_id=1, replica_groups=mesh['wide'=8,'narrow'=4] {'narrow'}, use_global_device_ids=true, to_apply=%region_12.13 | all-reduce | flops 768 | bytes 6144 | tf_op jit(solution)/shard_map/psum | solution.py:47
  77.8 0.6 subtract_reduce_fusion
  78.5 22.0 %all-reduce = (f32[]{:T(128)}, f32[]{:T(128)}) all-reduce(f32[]{:T(128)} %get-tuple-element.149, f32[]{:T(128)} %get-tuple-element.148), channel_id=1, replica_groups=mesh['wide'=8,'narrow'=4] {'wide'}, use_global_device_ids=true, to_apply=%region_7.8 | all-reduce | flops 2 | bytes 16 | tf_op jit(solution)/shard_map/psum | solution.py:50
  100.4 0.8 fusion.12
  101.3 1.5 convolution_multiply_fusion.1
  102.7 0.0 reduce-scatter.2.cloned.1.call-update
  104.1 0.2 convolution_multiply_fusion.3
  104.3 73.4 %while.15 = (s32[]{:T(128)}, f32[64,1024]{1,0:T(8,128)S(1)}, s32[]{:T(128)}, bf16[256,512]{0,1:T(8,128)(2,1)S(1)}, bf16[256,1024]{1,0:T(8,128)(2,1)S(1)}, /*inde...) while((s32[]{:T(128)}, f32[64,1024]{1,0:T(8,128)S(1)}, s32[]{:T(128)}, ...), condition=%wide.region_10.11_spmd, body=%wide.region_9.10_spmd.sunk | while | flops 33685520 | bytes 2130252 | solution.py:81
  104.3 0.1 collective-permute-start
  104.4 9.0 %collective-permute-done = f32[64,1024]{1,0:T(8,128)S(1)} collective-permute-done((f32[64,1024]{1,0:T(8,128)S(1)}, f32[64,1024]{1,0:T(8,128)S(1)}, u32[]{:S(2)}, u32[]{:S(2)}) %collective-permute-start) | collective-permute-done | bytes 262176 | tf_op jit(solution)/shard_map/while/body/eval_jaxpr/ppermute | solution.py:10
  113.4 0.2 fusion.27
  113.7 0.1 collective-permute-start
  113.8 9.7 %collective-permute-done = f32[64,1024]{1,0:T(8,128)S(1)} collective-permute-done((f32[64,1024]{1,0:T(8,128)S(1)}, f32[64,1024]{1,0:T(8,128)S(1)}, u32[]{:S(2)}, u32[]{:S(2)}) %collective-permute-start) | collective-permute-done | bytes 262176 | tf_op jit(solution)/shard_map/while/body/eval_jaxpr/ppermute | solution.py:10
  123.4 0.2 fusion.27
  123.6 0.1 collective-permute-start
  123.7 10.8 %collective-permute-done = f32[64,1024]{1,0:T(8,128)S(1)} collective-permute-done((f32[64,1024]{1,0:T(8,128)S(1)}, f32[64,1024]{1,0:T(8,128)S(1)}, u32[]{:S(2)}, u32[]{:S(2)}) %collective-permute-start) | collective-permute-done | bytes 262176 | tf_op jit(solution)/shard_map/while/body/eval_jaxpr/ppermute | solution.py:10
  134.5 0.2 fusion.27
  134.8 0.1 collective-permute-start
  134.9 11.7 %collective-permute-done = f32[64,1024]{1,0:T(8,128)S(1)} collective-permute-done((f32[64,1024]{1,0:T(8,128)S(1)}, f32[64,1024]{1,0:T(8,128)S(1)}, u32[]{:S(2)}, u32[]{:S(2)}) %collective-permute-start) | collective-permute-done | bytes 262176 | tf_op jit(solution)/shard_map/while/body/eval_jaxpr/ppermute | solution.py:10
  146.6 0.2 fusion.27
  146.8 0.1 collective-permute-start
  146.9 10.9 %collective-permute-done = f32[64,1024]{1,0:T(8,128)S(1)} collective-permute-done((f32[64,1024]{1,0:T(8,128)S(1)}, f32[64,1024]{1,0:T(8,128)S(1)}, u32[]{:S(2)}, u32[]{:S(2)}) %collective-permute-start) | collective-permute-done | bytes 262176 | tf_op jit(solution)/shard_map/while/body/eval_jaxpr/ppermute | solution.py:10
  157.8 0.2 fusion.27
  158.0 0.1 collective-permute-start
  158.1 10.0 %collective-permute-done = f32[64,1024]{1,0:T(8,128)S(1)} collective-permute-done((f32[64,1024]{1,0:T(8,128)S(1)}, f32[64,1024]{1,0:T(8,128)S(1)}, u32[]{:S(2)}, u32[]{:S(2)}) %collective-permute-start) | collective-permute-done | bytes 262176 | tf_op jit(solution)/shard_map/while/body/eval_jaxpr/ppermute | solution.py:10
  168.1 0.2 fusion.27
  168.3 0.1 collective-permute-start
  168.4 9.0 %collective-permute-done = f32[64,1024]{1,0:T(8,128)S(1)} collective-permute-done((f32[64,1024]{1,0:T(8,128)S(1)}, f32[64,1024]{1,0:T(8,128)S(1)}, u32[]{:S(2)}, u32[]{:S(2)}) %collective-permute-start) | collective-permute-done | bytes 262176 | tf_op jit(solution)/shard_map/while/body/eval_jaxpr/ppermute | solution.py:10
  177.5 0.2 fusion.27
  177.7 0.7 convert_element_type.15
  178.4 0.0 reduce-scatter.2.cloned.1.call-done
  178.4 1.6 convert_element_type.14
  (18 shorter events, 0.2 us)
Async XLA Ops:
  7.2 57.2 %copy-start = (bf16[64,1024]{1,0:T(8,128)(2,1)S(1)}, bf16[64,1024]{1,0:T(8,128)(2,1)}, u32[]{:S(2)}) copy-start(bf16[64,1024]{1,0:T(8,128)(2,1)} %param.6) | copy-start | bytes 393220
  7.2 171.2 %reduce-scatter.2.cloned.1.call-start = ((), (), s32[]{:S(2)}) async-start(), calls=%async_computation.1 | async-start | bytes 1310720 | tf_op jit(solution)/shard_map/reduce_scatter | solution.py:66
  7.2 9.8 %collective-permute-start.1 = (bf16[64,1024]{1,0:T(8,128)(2,1)}, bf16[64,1024]{1,0:T(8,128)(2,1)S(1)}, u32[]{:S(2)}, u32[]{:S(2)}) collective-permute-start(bf16[64,1024]{1,0:T(8,128)(2,1)} %param.6), channel_id=1, source_target_pairs={{0,4},{4,8},{8,12},{12,16},{16,20},{20,24},{24,28},{28,0},{1,5},{5... | collective-permute-start | bytes 393224 | tf_op jit(solution)/shard_map/ppermute | solution.py:27
  17.0 7.7 %collective-permute-start.2 = (bf16[64,1024]{1,0:T(8,128)(2,1)S(1)}, bf16[64,1024]{1,0:T(8,128)(2,1)S(1)}, u32[]{:S(2)}, u32[]{:S(2)}) collective-permute-start(bf16[64,1024]{1,0:T(8,128)(2,1)S(1)} %collective-permute-done.1), channel_id=1, source_target_pairs={{0,4},{4,8},{8,12},{12,16},{16,20},{20,24},{24,28},{28,0},{1,5},{5... | collective-permute-start | bytes 393224 | tf_op jit(solution)/shard_map/ppermute | solution.py:27
  24.7 7.7 %collective-permute-start.3 = (bf16[64,1024]{1,0:T(8,128)(2,1)S(1)}, bf16[64,1024]{1,0:T(8,128)(2,1)S(1)}, u32[]{:S(2)}, u32[]{:S(2)}) collective-permute-start(bf16[64,1024]{1,0:T(8,128)(2,1)S(1)} %collective-permute-done.2), channel_id=1, source_target_pairs={{0,4},{4,8},{8,12},{12,16},{16,20},{20,24},{24,28},{28,0},{1,5},{5... | collective-permute-start | bytes 393224 | tf_op jit(solution)/shard_map/ppermute | solution.py:27
  32.3 7.7 %collective-permute-start.4 = (bf16[64,1024]{1,0:T(8,128)(2,1)S(1)}, bf16[64,1024]{1,0:T(8,128)(2,1)S(1)}, u32[]{:S(2)}, u32[]{:S(2)}) collective-permute-start(bf16[64,1024]{1,0:T(8,128)(2,1)S(1)} %collective-permute-done.3), channel_id=1, source_target_pairs={{0,4},{4,8},{8,12},{12,16},{16,20},{20,24},{24,28},{28,0},{1,5},{5... | collective-permute-start | bytes 393224 | tf_op jit(solution)/shard_map/ppermute | solution.py:27
  40.0 7.7 %collective-permute-start.5 = (bf16[64,1024]{1,0:T(8,128)(2,1)S(1)}, bf16[64,1024]{1,0:T(8,128)(2,1)S(1)}, u32[]{:S(2)}, u32[]{:S(2)}) collective-permute-start(bf16[64,1024]{1,0:T(8,128)(2,1)S(1)} %collective-permute-done.4), channel_id=1, source_target_pairs={{0,4},{4,8},{8,12},{12,16},{16,20},{20,24},{24,28},{28,0},{1,5},{5... | collective-permute-start | bytes 393224 | tf_op jit(solution)/shard_map/ppermute | solution.py:27
  47.7 8.9 %collective-permute-start.6 = (bf16[64,1024]{1,0:T(8,128)(2,1)S(1)}, bf16[64,1024]{1,0:T(8,128)(2,1)S(1)}, u32[]{:S(2)}, u32[]{:S(2)}) collective-permute-start(bf16[64,1024]{1,0:T(8,128)(2,1)S(1)} %collective-permute-done.5), channel_id=1, source_target_pairs={{0,4},{4,8},{8,12},{12,16},{16,20},{20,24},{24,28},{28,0},{1,5},{5... | collective-permute-start | bytes 393224 | tf_op jit(solution)/shard_map/ppermute | solution.py:27
  56.6 7.7 %collective-permute-start.7 = (bf16[64,1024]{1,0:T(8,128)(2,1)S(1)}, bf16[64,1024]{1,0:T(8,128)(2,1)S(1)}, u32[]{:S(2)}, u32[]{:S(2)}) collective-permute-start(bf16[64,1024]{1,0:T(8,128)(2,1)S(1)} %collective-permute-done.6), channel_id=1, source_target_pairs={{0,4},{4,8},{8,12},{12,16},{16,20},{20,24},{24,28},{28,0},{1,5},{5... | collective-permute-start | bytes 393224 | tf_op jit(solution)/shard_map/ppermute | solution.py:27
  104.3 9.1 %collective-permute-start = (f32[64,1024]{1,0:T(8,128)S(1)}, f32[64,1024]{1,0:T(8,128)S(1)}, u32[]{:S(2)}, u32[]{:S(2)}) collective-permute-start(f32[64,1024]{1,0:T(8,128)S(1)} %get-tuple-element.211), channel_id=1, source_target_pairs={{0,4},{4,8},{8,12},{12,16},{16,20},{20,24},{24,28},{28,0},{1,5},{5... | collective-permute-start | bytes 786440 | tf_op jit(solution)/shard_map/while/body/eval_jaxpr/ppermute | solution.py:10
  113.7 9.7 %collective-permute-start = (f32[64,1024]{1,0:T(8,128)S(1)}, f32[64,1024]{1,0:T(8,128)S(1)}, u32[]{:S(2)}, u32[]{:S(2)}) collective-permute-start(f32[64,1024]{1,0:T(8,128)S(1)} %get-tuple-element.211), channel_id=1, source_target_pairs={{0,4},{4,8},{8,12},{12,16},{16,20},{20,24},{24,28},{28,0},{1,5},{5... | collective-permute-start | bytes 786440 | tf_op jit(solution)/shard_map/while/body/eval_jaxpr/ppermute | solution.py:10
  123.6 10.9 %collective-permute-start = (f32[64,1024]{1,0:T(8,128)S(1)}, f32[64,1024]{1,0:T(8,128)S(1)}, u32[]{:S(2)}, u32[]{:S(2)}) collective-permute-start(f32[64,1024]{1,0:T(8,128)S(1)} %get-tuple-element.211), channel_id=1, source_target_pairs={{0,4},{4,8},{8,12},{12,16},{16,20},{20,24},{24,28},{28,0},{1,5},{5... | collective-permute-start | bytes 786440 | tf_op jit(solution)/shard_map/while/body/eval_jaxpr/ppermute | solution.py:10
  134.8 11.8 %collective-permute-start = (f32[64,1024]{1,0:T(8,128)S(1)}, f32[64,1024]{1,0:T(8,128)S(1)}, u32[]{:S(2)}, u32[]{:S(2)}) collective-permute-start(f32[64,1024]{1,0:T(8,128)S(1)} %get-tuple-element.211), channel_id=1, source_target_pairs={{0,4},{4,8},{8,12},{12,16},{16,20},{20,24},{24,28},{28,0},{1,5},{5... | collective-permute-start | bytes 786440 | tf_op jit(solution)/shard_map/while/body/eval_jaxpr/ppermute | solution.py:10
  146.8 11.0 %collective-permute-start = (f32[64,1024]{1,0:T(8,128)S(1)}, f32[64,1024]{1,0:T(8,128)S(1)}, u32[]{:S(2)}, u32[]{:S(2)}) collective-permute-start(f32[64,1024]{1,0:T(8,128)S(1)} %get-tuple-element.211), channel_id=1, source_target_pairs={{0,4},{4,8},{8,12},{12,16},{16,20},{20,24},{24,28},{28,0},{1,5},{5... | collective-permute-start | bytes 786440 | tf_op jit(solution)/shard_map/while/body/eval_jaxpr/ppermute | solution.py:10
  158.0 10.1 %collective-permute-start = (f32[64,1024]{1,0:T(8,128)S(1)}, f32[64,1024]{1,0:T(8,128)S(1)}, u32[]{:S(2)}, u32[]{:S(2)}) collective-permute-start(f32[64,1024]{1,0:T(8,128)S(1)} %get-tuple-element.211), channel_id=1, source_target_pairs={{0,4},{4,8},{8,12},{12,16},{16,20},{20,24},{24,28},{28,0},{1,5},{5... | collective-permute-start | bytes 786440 | tf_op jit(solution)/shard_map/while/body/eval_jaxpr/ppermute | solution.py:10
  168.3 9.1 %collective-permute-start = (f32[64,1024]{1,0:T(8,128)S(1)}, f32[64,1024]{1,0:T(8,128)S(1)}, u32[]{:S(2)}, u32[]{:S(2)}) collective-permute-start(f32[64,1024]{1,0:T(8,128)S(1)} %get-tuple-element.211), channel_id=1, source_target_pairs={{0,4},{4,8},{8,12},{12,16},{16,20},{20,24},{24,28},{28,0},{1,5},{5... | collective-permute-start | bytes 786440 | tf_op jit(solution)/shard_map/while/body/eval_jaxpr/ppermute | solution.py:10
Sparse Core Ops, SparseCore 0:
  102.9 21.7 reduce-scatter.1
